TPU v7x, 128 devices: a whole 4x4x4 slice. The times are simulated.
128 devices in a mesh: shard: 8 (over y, core), model: 16 (over z, x).
Axes of the slice: x: 4, y: 4, z: 4, core: 2. Of those that a mesh axis runs over, the one named last changes fastest.
Arguments:
- train_gate: float32 [4096, 12288], P('shard', 'model'), may hold values from -0.125 to 0.125
- slow_gate: float32 [4096, 12288], P('shard', 'model'), may hold values from -0.09375 to 0.09375
- train_up: float32 [4096, 12288], P('shard', 'model'), may hold values from -0.125 to 0.125
- slow_up: float32 [4096, 12288], P('shard', 'model'), may hold values from -0.09375 to 0.09375
- norm_train: float32 [4096], P(('shard', 'model')), may hold values from 0.25 to 1.75
- norm_step: float32 [4096], P(('shard', 'model')), may hold values from -0.3 to 0.3
Outputs:
- serve_gate: bfloat16 [4096, 12288], P(None, 'model')
- serve_up: bfloat16 [4096, 12288], P(None, 'model')
- factor_gate: float32 [12288], P('model')
- factor_up: float32 [12288], P('model')
- serve_norm: bfloat16 [4096], replicated
- fresh_gate: float32 [4096, 12288], P('shard', 'model')
- fresh_up: float32 [4096, 12288], P('shard', 'model')
All inputs are finite; a program needn't handle non-finite values. Where the computation divides by a largest or mean magnitude, that divisor is 1e-20 or more.
Results may differ from a plain program's by a relative error of at most 0.001.
Values may be sent and summed in bfloat16 or wider, within the bound.
A program may use at most 128 MiB of HBM per device.

v0:
```python
import jax
import jax.numpy as jnp
from jax import lax
from jax.sharding import Mesh
from jax.sharding import PartitionSpec as P

D_MODEL = 4096
SHARD = ("shard_0", "shard_1")
SHARD_MODEL = ("shard_0", "shard_1", "model_0", "model_1")
MODEL = ("model_0", "model_1")


keep_rate = 0.75


def from_everyone(array, axis):
    copies = jnp.broadcast_to(array, (lax.axis_size(axis), *array.shape))
    return lax.all_to_all(copies, axis, split_axis=0, concat_axis=0, tiled=True)


def taken_together(array, axis):
    everything = from_everyone(array, axis)
    return jnp.sum(everything, axis=0)


def in_one(arrays, axis):
    ends = [0]
    for a in arrays:
        ends.append(ends[-1] + a.size)
    subtotal = taken_together(jnp.concatenate([a.ravel() for a in arrays]), axis)
    return tuple((subtotal[b:e].reshape(a.shape) for a, b, e in zip(arrays, ends, ends[1:])))


def sent_together(arrays, axis, dim, along):
    widths = [a.shape[along] for a in arrays]
    both = jnp.concatenate(arrays, axis=along)
    filled = lax.all_gather(both, axis, axis=dim, tiled=True)
    return tuple(jnp.split(filled, [sum(widths[:k]) for k in range(1, len(widths))], axis=along))


def in_order(blocks, dim):
    blocks = jnp.moveaxis(blocks, 0, dim)
    lengths = blocks.shape
    return blocks.reshape(*lengths[:dim], lengths[dim] * lengths[dim + 1], *lengths[dim + 2 :])


def stacked_from(array, axes, turns):
    blocks = array[None]
    for k in turns:
        blocks = lax.all_gather(blocks, axes[k], axis=0, tiled=True)
    held = [lax.axis_size(axes[k]) for k in reversed(turns)]
    blocks = blocks.reshape(*held, *array.shape)
    turned = sorted(range(len(turns)), key=lambda place: turns[len(turns) - 1 - place])
    return blocks.transpose(*turned, *range(len(turns), blocks.ndim)).reshape(-1, *array.shape)


def gathered_by_axis(array, axes, turns, dim):
    return in_order(stacked_from(array, axes, turns), dim)


def shards(train_gate, slow_gate, train_up, slow_up, norm_train, norm_step):
    fresh_gate = keep_rate * slow_gate + (1.0 - keep_rate) * train_gate
    fresh_up = keep_rate * slow_up + (1.0 - keep_rate) * train_up
    total_gate, total_up = in_one(
        (jnp.sum(jnp.abs(fresh_gate), axis=0), jnp.sum(jnp.abs(fresh_up), axis=0)), SHARD
    )
    factor_gate = total_gate / D_MODEL
    factor_up = total_up / D_MODEL
    narrow_gate, narrow_up = (
        (fresh_gate / factor_gate).astype(jnp.bfloat16),
        (fresh_up / factor_up).astype(jnp.bfloat16),
    )
    serve_gate, serve_up = sent_together((narrow_gate, narrow_up), SHARD, 0, 1)
    serve_norm = gathered_by_axis(
        (norm_train + norm_step).astype(jnp.bfloat16), SHARD_MODEL, (0, 2, 3, 1), 0
    )
    return (serve_gate, serve_up, factor_gate, factor_up, serve_norm, fresh_gate, fresh_up)


def solution(mesh):
    split = Mesh(mesh.devices.reshape(4, 2, 4, 4), ("shard_0", "shard_1", "model_0", "model_1"))
    return jax.shard_map(
        shards,
        mesh=split,
        in_specs=(
            P(SHARD, MODEL),
            P(SHARD, MODEL),
            P(SHARD, MODEL),
            P(SHARD, MODEL),
            P(SHARD_MODEL),
            P(SHARD_MODEL),
        ),
        out_specs=(
            P(None, MODEL),
            P(None, MODEL),
            P(MODEL),
            P(MODEL),
            P(),
            P(SHARD, MODEL),
            P(SHARD, MODEL),
        ),
        check_vma=False,
    )
```

profile of v0, /device:TPU:1, one launch (start us, length us, event | category | flops | bytes accessed | tf_op | source)
XLA Modules:
  0.0 108.5 jit_solution(1710898650069235913)
XLA Ops:
  7.2 0.0 all-gather.5.cloned.1.call-start
  7.2 3.4 %abs_reduce_fusion = (f32[768]{0:T(1024)S(1)}, f32[512,768]{1,0:T(8,128)S(1)}, f32[768]{0:T(1024)S(1)}, f32[512,768]{1,0:T(8,128)S(1)}) fusion(f32[512,768]{1,0:T(8,128)} %param.8, f32[512,768]{1,0:T(8,128)} %param.9, f32[512,768]{1,0:T(8,128)} %param.6, f32[512,768]{1,0:T(8,128)} %param.7), kind=kLoop, calls=%fused_computation.3 | loop fusion | flops 3930624 | bytes 9443328 | tf_op jit(solution)/shard_map/reduce_sum | solution.py:65
  10.6 0.0 copy-start
  10.6 10.5 %all_to_all.6 = f32[8,1,1536]{2,1,0:T(1,128)S(1)} all-to-all(f32[8,1,1536]{2,1,0:T(1,128)S(1)} %broadcast_in_dim.8), channel_id=1, replica_groups=mesh['shard_0'=4,'shard_1'=2,'model_0'=4,'model_1'=4] {'shard_0','shard_1'}, dimensions={0} | all-to-all | bytes 98304 | tf_op jit(solution)/shard_map/all_to_all | solution.py:18
  21.2 0.0 copy-start.2
  21.3 0.1 divide_convert_fusion.1
  21.4 0.1 divide_convert_fusion
  21.5 0.3 copy-done.2
  21.8 0.0 copy-done.3
  21.9 1.3 %pad_maximum_fusion = bf16[512,1536]{1,0:T(8,128)(2,1)} fusion(bf16[512,768]{1,0:T(8,128)(2,1)S(1)} %divide_convert_fusion, bf16[512,768]{1,0:T(8,128)(2,1)S(1)} %divide_convert_fusion.1), kind=kLoop, calls=%fused_computation | loop fusion | flops 3145728 | bytes 3145728 | tf_op jit(solution)/shard_map/concatenate | solution.py:36
  23.1 0.0 all-gather.5.cloned.1.call-update
  23.2 0.6 copy-done.6
  23.8 0.6 dynamic-slice
  25.1 0.2 dynamic-update-slice
  25.3 6.9 %all-reduce = bf16[128]{0:T(256)(128)(2,1)S(1)} all-reduce(bf16[128]{0:T(256)(128)(2,1)S(1)} %dynamic-update-slice), channel_id=2, replica_groups=mesh['shard_0'=4,'shard_1'=2,'model_0'=4,'model_1'=4] {'shard_0'}, use_global_device_ids=true, to_apply=%add | all-reduce | flops 128 | bytes 512
  32.2 0.1 reshape.28
  32.2 9.4 %all-gather.1 = bf16[4,4,32]{2,1,0:T(4,128)(2,1)S(1)} all-gather(bf16[1,4,32]{2,1,0:T(4,128)(2,1)S(1)} %reshape.28), channel_id=1, replica_groups=mesh['shard_0'=4,'shard_1'=2,'model_0'=4,'model_1'=4] {'model_0'}, dimensions={0}, use_global_device_ids=true | all-gather | bytes 1280 | tf_op jit(solution)/shard_map/all_gather | solution.py:50
  41.6 10.4 %all_gather.18 = bf16[64,32]{1,0:T(8,128)(2,1)S(1)} all-gather(bf16[16,32]{1,0:T(8,128)(2,1)S(1)} %bitcast.8), channel_id=1, replica_groups=mesh['shard_0'=4,'shard_1'=2,'model_0'=4,'model_1'=4] {'model_1'}, dimensions={0}, use_global_device_ids=true | all-gather | bytes 5120 | tf_op jit(solution)/shard_map/all_gather | solution.py:50
  52.0 0.1 copy.24
  52.1 7.8 %all-gather.2 = bf16[2,64,32]{1,2,0:T(8,128)(2,1)S(1)} all-gather(bf16[1,64,32]{1,2,0:T(8,128)(2,1)S(1)} %copy.24), channel_id=1, replica_groups=mesh['shard_0'=4,'shard_1'=2,'model_0'=4,'model_1'=4] {'shard_1'}, dimensions={0}, use_global_device_ids=true | all-gather | bytes 12288 | tf_op jit(solution)/shard_map/all_gather | solution.py:50
  59.9 0.1 copy.25
  60.0 0.7 reshape_reshape.3
  60.7 30.7 %all-gather.5.cloned.1.call-done = bf16[4096,1536]{1,0:T(8,128)(2,1)} async-done(((bf16[512,1536]{1,0:T(8,128)(2,1)}), bf16[4096,1536]{1,0:T(8,128)(2,1)}) %all-gather.5.cloned.1.call-update) | async-done | bytes 12582928 | tf_op jit(solution)/shard_map/all_gather | solution.py:37
  91.4 10.2 %fusion = (bf16[4096,768]{1,0:T(8,128)(2,1)}, bf16[4096,768]{1,0:T(8,128)(2,1)}) fusion(bf16[4096,1536]{1,0:T(8,128)(2,1)} %all-gather.5.cloned.1.call-done), kind=kLoop, calls=%fused_computation.11 | loop fusion | bytes 25165824 | tf_op jit(solution)/shard_map/split | solution.py:38
  (16 shorter events, 0.1 us)
Async XLA Ops:
  7.2 84.3 %all-gather.5.cloned.1.call-start = ((), (), s32[]{:S(2)}) async-start(), calls=%async_computation.1 | async-start | bytes 14155776 | tf_op jit(solution)/shard_map/all_gather | solution.py:37
  10.6 11.0 %copy-start = (f32[512,768]{1,0:T(8,128)}, f32[512,768]{1,0:T(8,128)S(1)}, u32[]{:S(2)}) copy-start(f32[512,768]{1,0:T(8,128)S(1)} %get-tuple-element.10) | copy-start | bytes 4718596
  10.6 11.0 %copy-start.1 = (f32[512,768]{1,0:T(8,128)}, f32[512,768]{1,0:T(8,128)S(1)}, u32[]{:S(2)}) copy-start(f32[512,768]{1,0:T(8,128)S(1)} %get-tuple-element.16) | copy-start | bytes 4718596
  21.2 0.6 copy-start.2
  21.3 0.6 copy-start.3
  23.1 0.7 copy-start.6
  23.1 1.9 %copy-start.4 = (f32[32]{0:T(128)S(1)}, f32[32]{0:T(128)}, u32[]{:S(2)}) copy-start(f32[32]{0:T(128)} %param.10) | copy-start | bytes 388
  23.1 1.9 %copy-start.5 = (f32[32]{0:T(128)S(1)}, f32[32]{0:T(128)}, u32[]{:S(2)}) copy-start(f32[32]{0:T(128)} %param.11) | copy-start | bytes 388
Sparse Core Ops, SparseCore 0:
  23.3 68.1 all-gather.4
where the time goes:
time: 109 us
  blocking collectives  45 us (41%)
  waiting for transfers between devices  30.7 us (28%)
  between operations  14.8 us (14%)
  local copies, waits for them, and re-layouts  13 us (12%)
  other arithmetic  4.91 us (5%)
    all_gather x1, waiting for transfers between devices, sent_together(): filled = lax.all_gather(both, axis, axis=dim, tiled=True)  30.7 us
    all_gather x3, blocking collectives, stacked_from(): blocks = lax.all_gather(blocks, axes[k], axis=0, tiled=True)  27.6 us
    all_to_all x1, blocking collectives, from_everyone(): return lax.all_to_all(copies, axis, split_axis=0, concat_axis=0, tiled=True)  10.5 us
    split x1, local copies, waits for them, and re-layouts, sent_together(): jnp.split(filled, [sum(widths[:k]) for k in range(1, len(widths))], axis=...  10.2 us
    unnamed x1, blocking collectives  6.85 us
    reduce_sum x1, other arithmetic, shards(): jnp.sum(jnp.abs(fresh_up), axis=0)  3.36 us
  transfers between devices with their start and end apart: 1, of which 1 were waited for; matrix products, arithmetic and copies ran while one was open for 2% of the time, Pallas kernels for 0%

commit v1 on v0

v1 whole, which is shorter than its diff:
```python
import jax
import jax.numpy as jnp
from jax import lax
from jax.experimental import pallas as pl
from jax.experimental.pallas import tpu as pltpu
from jax.sharding import PartitionSpec as P

KEEP = 0.75
MESH = pl.DeviceIdType.MESH
LANES = 128


def dma(shape=()):
    return pltpu.SemaphoreType.DMA(shape)


def gather_kernel(
    tg, sg, tu, su, nt, ns,
    out_g, out_u, fresh_g, fresh_u, fac_g, fac_u, norm_out,
    stage_t, stage_s, gains, sums0, sums1, norm1, norm2, norm32,
    in_t, in_s, in_n, ex_send, ex_recv, own_send, own_recv, relay_send, relay_recv,
    mate_send, mate_recv, nsend, nrecv,
):
    rows, cols = fresh_g.shape
    per = cols // LANES
    n_blocks = 2 * per
    d_model = out_g.shape[0]
    s = lax.axis_index("shard")
    m = lax.axis_index("model")
    y, c = s // 2, s % 2
    right = ((y + 1) % 4) * 2 + c
    left = ((y + 3) % 4) * 2 + c
    far = ((y + 2) % 4) * 2 + c
    mate = y * 2 + (1 - c)
    z, x = m // 4, m % 4
    source = ((tg, sg), (tu, su))
    fresh = (fresh_g, fresh_u)
    out = (out_g, out_u)
    fac = (fac_g, fac_u)

    def columns(k):
        return k // per, pl.ds((k % per) * LANES, LANES)

    def loads(k):
        a, at = columns(k)
        return (
            pltpu.make_async_copy(source[a][0].at[:, at], stage_t.at[k], in_t.at[k]),
            pltpu.make_async_copy(source[a][1].at[:, at], stage_s.at[k], in_s.at[k]),
        )

    for k in range(n_blocks):
        for copy in loads(k):
            copy.start()
    gain_loads = [
        pltpu.make_async_copy(nt, gains.at[0], in_n.at[0]),
        pltpu.make_async_copy(ns, gains.at[1], in_n.at[1]),
    ]
    for copy in gain_loads:
        copy.start()

    barrier = pltpu.get_barrier_semaphore()
    shard_peers = [(s + d) % 8 for d in range(1, 8)]
    x_peers = [z * 4 + (x + d) % 4 for d in range(1, 4)]
    z_peers = [((z + d) % 4) * 4 + x for d in range(1, 4)]
    for p in shard_peers:
        pl.semaphore_signal(barrier, inc=1, device_id=(p, m), device_id_type=MESH)
    for p in x_peers + z_peers:
        pl.semaphore_signal(barrier, inc=1, device_id=(s, p), device_id_type=MESH)

    def block_sum(k):
        a, at = columns(k)
        for copy in loads(k):
            copy.wait()

        def step(i, total):
            r = pl.multiple_of(i * 64, 64)
            value = KEEP * stage_s[k, pl.ds(r, 64), :] + (1.0 - KEEP) * stage_t[k, pl.ds(r, 64), :]
            fresh[a][pl.ds(r, 64), at] = value
            return total + jnp.sum(jnp.abs(value).reshape(8, 8, LANES), axis=0)

        total = lax.fori_loop(0, rows // 64, step, jnp.zeros((8, LANES), jnp.float32))
        return jnp.sum(total, axis=0, keepdims=True)

    def exchange(g, buffer):
        return [
            pltpu.make_async_remote_copy(
                src_ref=buffer.at[s],
                dst_ref=buffer.at[s],
                send_sem=ex_send.at[g, p],
                recv_sem=ex_recv.at[g, s],
                device_id=(p, m),
                device_id_type=MESH,
            )
            for p in shard_peers
        ]

    def arrivals(g, buffer):
        for p in shard_peers:
            pltpu.make_async_remote_copy(
                src_ref=buffer.at[p],
                dst_ref=buffer.at[p],
                send_sem=ex_send.at[g, p],
                recv_sem=ex_recv.at[g, p],
                device_id=(p, m),
                device_id_type=MESH,
            ).wait_recv()

    def norm_row():
        for copy in gain_loads:
            copy.wait()
        norm1[s] = jnp.zeros((1, LANES), jnp.float32)
        norm1[s, :, 0:32] = gains[0] + gains[1]

    def block_at(k, owner):
        a, at = columns(k)
        return out[a].at[pl.ds(pl.multiple_of(owner * rows, rows), rows), at]

    def sent(k, owner, send, recv, to):
        block = block_at(k, owner)
        return pltpu.make_async_remote_copy(
            src_ref=block,
            dst_ref=block,
            send_sem=send,
            recv_sem=recv,
            device_id=(to, m),
            device_id_type=MESH,
        )

    def own(k, way):
        to = right if way == 0 else left
        return sent(k, s, own_send.at[way, k], own_recv.at[way, k], to)

    def landed(k, way):
        owner = left if way == 0 else right
        return sent(k, owner, own_send.at[way, k], own_recv.at[way, k], right)

    def relay(k, way):
        owner, to = (left, right) if way == 0 else (right, left)
        return sent(k, owner, relay_send.at[k], relay_recv.at[k], to)

    def relayed(k):
        return sent(k, far, relay_send.at[k], relay_recv.at[k], right)

    def to_mate(k, kind):
        owner = (s, left, right, far)[kind]
        return sent(k, owner, mate_send.at[kind, k], mate_recv.at[kind, k], mate)

    def from_mate(k, kind):
        base = (mate, left + 1 - 2 * c, right + 1 - 2 * c, far + 1 - 2 * c)[kind]
        return sent(k, base, mate_send.at[kind, k], mate_recv.at[kind, k], mate)

    def scale(k, row):
        a, at = columns(k)
        factor = row / d_model
        fac[a][k % per : k % per + 1, :] = factor
        inverse = 1.0 / factor
        start = pl.multiple_of(s * rows, rows)

        def step(i, carry):
            r = pl.multiple_of(i * 64, 64)
            value = fresh[a][pl.ds(r, 64), at] * inverse
            out[a][pl.ds(start + r, 64), at] = value.astype(out_g.dtype)
            return carry

        lax.fori_loop(0, rows // 64, step, 0)

    sums0[s] = block_sum(0)
    norm_row()
    pl.semaphore_wait(barrier, 13)
    for copy in exchange(0, sums0):
        copy.start()
    for k in range(1, n_blocks):
        sums1[s, k - 1 : k, :] = block_sum(k)
    for copy in exchange(1, sums1):
        copy.start()

    arrivals(0, sums0)
    row0 = sums0[0]
    for i in range(1, 8):
        row0 = row0 + sums0[i]
    scale(0, row0)
    for way in (0, 1):
        own(0, way).start()
    to_mate(0, 0).start()

    arrivals(1, sums1)
    rest = sums1[0]
    for i in range(1, 8):
        rest = rest + sums1[i]
    right_order = list(range(n_blocks))
    left_order = [0] + list(range(per, n_blocks)) + list(range(1, per))
    scaled = {0}
    for kr, kl in zip(right_order[1:], left_order[1:]):
        for k in (kr, kl):
            if k not in scaled:
                scale(k, rest[k - 1 : k, :])
                scaled.add(k)
        own(kr, 0).start()
        own(kl, 1).start()
        to_mate(kr, 0).start()

    def norm_copy(ref, i, to):
        return pltpu.make_async_remote_copy(
            src_ref=ref,
            dst_ref=ref,
            send_sem=nsend.at[i],
            recv_sem=nrecv.at[i],
            device_id=to,
            device_id_type=MESH,
        )

    for d, p in enumerate(shard_peers):
        norm_copy(norm1.at[s], d, (p, m)).start()
    for d in range(1, 8):
        p = (s + 8 - d) % 8
        norm_copy(norm1.at[p], d - 1, (p, m)).wait_recv()
    lane_row = lax.broadcasted_iota(jnp.int32, (8, LANES), 0)
    tile = jnp.zeros((8, LANES), jnp.float32)
    for i in range(8):
        tile = jnp.where(lane_row == i, norm1[i], tile)
    norm2[m] = tile
    for d, p in enumerate(x_peers):
        norm_copy(norm2.at[m], 7 + d, (s, p)).start()

    for j in range(n_blocks):
        k = right_order[j]
        landed(k, 0).wait_recv()
        if k < per:
            relay(k, 0).start()
        to_mate(k, 1).start()
        k = left_order[j]
        landed(k, 1).wait_recv()
        if k >= per:
            relay(k, 1).start()
        to_mate(k, 2).start()
        if j == 0:
            for d in range(1, 4):
                p = z * 4 + (x + 4 - d) % 4
                norm_copy(norm2.at[p], 6 + d, (s, p)).wait_recv()
            for d, p in enumerate(z_peers):
                norm_copy(norm2.at[pl.ds(z * 4, 4)], 10 + d, (s, p)).start()
        if j == 1:
            for d in range(1, 4):
                pz = (z + 4 - d) % 4
                norm_copy(norm2.at[pl.ds(pz * 4, 4)], 9 + d, (s, pz * 4 + x)).wait_recv()
            for zz in range(4):
                line = norm2[zz * 4]
                for xx in range(1, 4):
                    line = line + pltpu.roll(norm2[zz * 4 + xx], 32 * xx, 1)
                norm32[pl.ds(zz, 8, stride=4), :] = line
            norm_out[...] = norm32[...].astype(norm_out.dtype)

    for j in range(per):
        for k in (j, per + j):
            relayed(k).wait_recv()
            to_mate(k, 3).start()

    for g, buffer in ((0, sums0), (1, sums1)):
        for copy in exchange(g, buffer):
            copy.wait_send()
    for d, p in enumerate(shard_peers):
        norm_copy(norm1.at[s], d, (p, m)).wait_send()
    for d, p in enumerate(x_peers):
        norm_copy(norm2.at[m], 7 + d, (s, p)).wait_send()
    for d, p in enumerate(z_peers):
        norm_copy(norm2.at[pl.ds(z * 4, 4)], 10 + d, (s, p)).wait_send()
    for k in range(n_blocks):
        own(k, 0).wait_send()
        own(k, 1).wait_send()
        relay(k, 0 if k < per else 1).wait_send()
        for kind in range(4):
            to_mate(k, kind).wait_send()
    for k in range(n_blocks):
        for kind in range(4):
            from_mate(k, kind).wait_recv()


def write_kernel(*refs):
    ins, outs, sem = refs[:7], refs[7:14], refs[14]
    copies = []
    for a, b in zip(ins, outs):
        parts = 4 if a.shape[0] % 512 == 0 else 1
        size = a.shape[0] // parts
        for i in range(parts):
            at = pl.ds(i * size, size)
            copies.append(
                pltpu.make_async_copy(a.at[at], b.at[at], sem.at[len(copies)])
            )
    for copy in copies:
        copy.start()
    for copy in copies:
        copy.wait()


def body(tg, sg, tu, su, nt, ns):
    rows, cols = tg.shape
    d_model = rows * 8
    blocks = 2 * cols // LANES
    hbm = pl.BlockSpec(memory_space=pltpu.HBM)
    vmem = pl.BlockSpec(memory_space=pltpu.VMEM)
    shapes = (
        ((d_model, cols), jnp.bfloat16),
        ((d_model, cols), jnp.bfloat16),
        ((rows, cols), jnp.float32),
        ((rows, cols), jnp.float32),
        ((cols // LANES, LANES), jnp.float32),
        ((cols // LANES, LANES), jnp.float32),
        ((32, LANES), jnp.bfloat16),
    )
    given = [
        pltpu.with_memory_space_constraint(a, pltpu.HBM)
        for a in (tg, sg, tu, su, nt.reshape(1, 32), ns.reshape(1, 32))
    ]
    gathered = pl.pallas_call(
        gather_kernel,
        out_shape=[pltpu.VMEM(*a) for a in shapes],
        in_specs=[hbm] * 6,
        out_specs=[vmem] * 7,
        scratch_shapes=[
            pltpu.VMEM((blocks, rows, LANES), jnp.float32),
            pltpu.VMEM((blocks, rows, LANES), jnp.float32),
            pltpu.VMEM((2, 1, 32), jnp.float32),
            pltpu.VMEM((8, 1, LANES), jnp.float32),
            pltpu.VMEM((8, 16, LANES), jnp.float32),
            pltpu.VMEM((8, 1, LANES), jnp.float32),
            pltpu.VMEM((16, 8, LANES), jnp.float32),
            pltpu.VMEM((32, LANES), jnp.float32),
            dma((blocks,)),
            dma((blocks,)),
            dma((2,)),
            dma((2, 8)),
            dma((2, 8)),
            dma((2, blocks)),
            dma((2, blocks)),
            dma((blocks,)),
            dma((blocks,)),
            dma((4, blocks)),
            dma((4, blocks)),
            dma((13,)),
            dma((13,)),
        ],
        compiler_params=pltpu.CompilerParams(
            collective_id=0, has_side_effects=True, vmem_limit_bytes=32 << 20
        ),
    )(*given)
    written = pl.pallas_call(
        write_kernel,
        out_shape=[jax.ShapeDtypeStruct(*a) for a in shapes],
        in_specs=[vmem] * 7,
        out_specs=[hbm] * 7,
        scratch_shapes=[dma((20,))],
        compiler_params=pltpu.CompilerParams(vmem_limit_bytes=16 << 20),
    )(*gathered)
    g, u, fg, fu, cg, cu, norm = written
    return g, u, cg.reshape(cols), cu.reshape(cols), norm.reshape(d_model), fg, fu


def solution(mesh):
    spread = P("shard", "model")
    return jax.shard_map(
        body,
        mesh=mesh,
        in_specs=(spread,) * 4 + (P(("shard", "model")),) * 2,
        out_specs=(
            P(None, "model"), P(None, "model"), P("model"), P("model"), P(), spread, spread,
        ),
        check_vma=False,
    )
```

time: 109 us -> 78.9 us (0.72)
  Pallas kernels: 0 us -> 78.2 us
  blocking collectives: 45 us -> 0 us
  waiting for transfers between devices: 30.7 us -> 0 us
  between operations: 14.8 us -> 0.64 us
  local copies, waits for them, and re-layouts: 13 us -> 0 us
  other arithmetic: 4.91 us -> 0 us
    pallas_call x0 -> x2, Pallas kernels: none -> 78.2 us  [the longest x1 72.5 us: body(): pl.pallas_call(gather_kernel, out_shape=[pltpu.VMEM(*a) for a in shapes],...]
    all_gather x1 -> x0, waiting for transfers between devices: 30.7 us -> none  [sent_together(): filled = lax.all_gather(both, axis, axis=dim, tiled=True)]
    all_gather x3 -> x0, blocking collectives: 27.6 us -> none  [stacked_from(): blocks = lax.all_gather(blocks, axes[k], axis=0, tiled=True)]
    all_to_all x1 -> x0, blocking collectives: 10.5 us -> none  [from_everyone(): return lax.all_to_all(copies, axis, split_axis=0, concat_axis=0, tiled=True)]
    split x1 -> x0, local copies, waits for them, and re-layouts: 10.2 us -> none  [sent_together(): jnp.split(filled, [sum(widths[:k]) for k in range(1, len(widths))], axis=...]
    unnamed x1 -> x0, blocking collectives: 6.85 us -> none
    reduce_sum x2 -> x0, other arithmetic: 3.4 us -> none  [the longest x1 3.36 us: shards(): jnp.sum(jnp.abs(fresh_up), axis=0)]
    unnamed x19 -> x0, local copies, waits for them, and re-layouts: 1.96 us -> none
  transfers between devices with their start and end apart: 1 -> 0, of which waited for: 1 -> 0; matrix products, arithmetic and copies ran while one was open for 2% -> 0% of each run, Pallas kernels for 0% -> 0%
where the time goes in v1:
time: 78.9 us; the launch traced here: 78.8 us
  Pallas kernels  78.2 us (99%)
    pallas_call x1, Pallas kernels, body(): pl.pallas_call(gather_kernel, out_shape=[pltpu.VMEM(*a) for a in shapes],...  72.5 us
    pallas_call x1, Pallas kernels, body(): pl.pallas_call(write_kernel, out_shape=[jax.ShapeDtypeStruct(*a) for a in...  5.68 us

profile of v1, /device:TPU:1, one launch (start us, length us, event | category | flops | bytes accessed | tf_op | source)
XLA Modules:
  0.0 78.8 jit_solution(7470316978300249936)
XLA Ops:
  0.6 72.5 %shard_map.117 = (bf16[4096,768]{1,0:T(8,128)(2,1)S(1)}, bf16[4096,768]{1,0:T(8,128)(2,1)S(1)}, f32[512,768]{1,0:T(8,128)S(1)}, f32[512,768]{1,0:T(8,128)S(1)}, ...) custom-call(f32[512,768]{1,0:T(8,128)} %tg.1, f32[512,768]{1,0:T(8,128)} %sg.1, ...), custom_call_target="tpu_custom_call" | custom-call | tf_op jit(solution)/shard_map/pallas_call | solution.py:314
  73.2 5.7 %shard_map.118 = (bf16[4096,768]{1,0:T(8,128)(2,1)}, bf16[4096,768]{1,0:T(8,128)(2,1)}, f32[512,768]{1,0:T(8,128)}, f32[512,768]{1,0:T(8,128)}, f32[6,128]{1,0:T...) custom-call(bf16[4096,768]{1,0:T(8,128)(2,1)S(1)} %get-tuple-element.21.refs_0_, ...), custom_call_target="tpu_custom_call" | custom-call | tf_op jit(solution)/shard_map/pallas_call | solution.py:346

commit v2 on v0

v2 whole, which is shorter than its diff:
```python
import jax
import jax.numpy as jnp
from jax import lax
from jax.experimental import pallas as pl
from jax.experimental.pallas import tpu as pltpu
from jax.sharding import PartitionSpec as P

KEEP = 0.75
MESH = pl.DeviceIdType.MESH
LANES = 128
FIRST = 128
UNITS = (
    (0, 0, 512, 0, FIRST),
    (0, 0, 320, FIRST, 768 - FIRST),
    (0, 320, 160, FIRST, 768 - FIRST),
    (0, 480, 32, FIRST, 768 - FIRST),
    (1, 0, 320, 0, 768),
    (1, 320, 160, 0, 768),
    (1, 480, 32, 0, 768),
)
RIGHT, LEFT = (0, 1, 2, 3, 4, 5, 6), (0, 4, 5, 6, 1, 2, 3)
RELAYED_RIGHT, RELAYED_LEFT = (0, 1, 2, 3), (4, 5, 6)


def dma(shape=()):
    return pltpu.SemaphoreType.DMA(shape)


def by_arrival(*queues):
    arrivals = []
    for way, units in queues:
        total = 0
        for u in units:
            total += UNITS[u][2] * UNITS[u][4]
            arrivals.append((total, way, u))
    return [(way, u) for _, way, u in sorted(arrivals)]


def gather_kernel(
    tg, sg, tu, su, nt, ns,
    out_g, out_u, fresh_g, fresh_u, fac_g, fac_u, norm_out,
    stage_g, stage_u, gains, sums0, sums1, norm1, norm2, norm32,
    in_sem, gain_sem, go, ex_send, ex_recv, own_send, own_recv, relay_send, relay_recv,
    mate_send, mate_recv, nsend, nrecv,
):
    rows, cols = fresh_g.shape
    d_model = out_g.shape[0]
    rest = cols - FIRST
    s = lax.axis_index("shard")
    m = lax.axis_index("model")
    y, c = s // 2, s % 2
    right = ((y + 1) % 4) * 2 + c
    left = ((y + 3) % 4) * 2 + c
    far = ((y + 2) % 4) * 2 + c
    mate = y * 2 + (1 - c)
    z, x = m // 4, m % 4
    fresh, out, fac, stage = (fresh_g, fresh_u), (out_g, out_u), (fac_g, fac_u), (stage_g, stage_u)
    shard_peers = [(s + d) % 8 for d in range(1, 8)]
    cross_peers = [z * 4 + (x + d) % 4 for d in range(1, 4)]
    cross_peers += [((z + d) % 4) * 4 + x for d in range(1, 4)]

    barrier = pltpu.get_barrier_semaphore()
    for d in range(1, 4):
        pl.semaphore_signal(
            barrier, inc=1, device_id=(((y + d) % 4) * 2 + 1, m), device_id_type=MESH
        )

    @pl.when(c == 0)
    def _():
        pl.semaphore_signal(barrier, inc=1, device_id=(mate, m), device_id_type=MESH)
        for p in cross_peers:
            pl.semaphore_signal(barrier, inc=1, device_id=(s, p), device_id_type=MESH)

    parts = ((0, 0, rows, 0, FIRST), (0, 0, rows, FIRST, rest), (1, 0, rows // 2, 0, cols), (1, rows // 2, rows // 2, 0, cols))
    for i, (a, r, nr, q, nq) in enumerate(parts):
        for kind, ref in enumerate(((sg, tg), (su, tu))[a]):
            pltpu.make_async_copy(
                ref.at[pl.ds(r, nr), pl.ds(q, nq)],
                stage[a].at[kind, pl.ds(r, nr), pl.ds(q, nq)],
                in_sem.at[i],
            ).start()
    for i, ref in enumerate((nt, ns)):
        pltpu.make_async_copy(ref, gains.at[i], gain_sem).start()

    def settle(ref, sem):
        pltpu.make_async_copy(ref, ref, sem).wait()

    def averaged(i, step, total):
        a, r0, nr, q, nq = parts[i]
        settle(stage[a].at[:, pl.ds(r0, nr), pl.ds(q, nq)], in_sem.at[i])
        at = pl.ds(q, nq)

        def one(j, total):
            r = pl.ds(pl.multiple_of(r0 + j * step, step), step)
            value = KEEP * stage[a][0, r, at] + (1.0 - KEEP) * stage[a][1, r, at]
            fresh[a][r, at] = value
            return total + jnp.sum(jnp.abs(value).reshape(step // 8, 8, nq), axis=0)

        return lax.fori_loop(0, nr // step, one, total)

    def collapsed(total):
        return jnp.sum(total, axis=0, keepdims=True)

    def exchange(g, buffer):
        for p in shard_peers:
            pltpu.make_async_remote_copy(
                src_ref=buffer.at[s],
                dst_ref=buffer.at[s],
                send_sem=ex_send.at[g],
                recv_sem=ex_recv.at[g],
                device_id=(p, m),
                device_id_type=MESH,
            ).start()

    def summed(g, buffer):
        settle(buffer.at[pl.ds(0, 7)], ex_recv.at[g])
        total = buffer[0]
        for i in range(1, 8):
            total = total + buffer[i]
        return total / d_model

    def unit_at(u, owner):
        a, r, nr, q, nq = UNITS[u]
        return out[a].at[pl.ds(pl.multiple_of(owner * rows + r, 32), nr), pl.ds(q, nq)]

    def sent(u, owner, send, recv, to):
        ref = unit_at(u, owner)
        return pltpu.make_async_remote_copy(
            src_ref=ref, dst_ref=ref, send_sem=send, recv_sem=recv, device_id=(to, m), device_id_type=MESH,
        )

    def own(u, way):
        sent(u, s, own_send, own_recv.at[way, u], (right, left)[way]).start()

    def landed(u, way):
        sent(u, (left, right)[way], own_send, own_recv.at[way, u], right).wait_recv()

    def relay(u, way):
        sent(u, (left, right)[way], relay_send, relay_recv.at[u], (right, left)[way]).start()

    def relayed(u):
        sent(u, far, relay_send, relay_recv.at[u], right).wait_recv()

    def to_mate(u, owner):
        sent(u, owner, mate_send, mate_recv, mate).start()

    def scale(u, inverse):
        a, r0, nr, q, nq = UNITS[u]
        at = pl.ds(q, nq)

        def one(j, carry):
            r = pl.multiple_of(r0 + j * 32, 32)
            value = fresh[a][pl.ds(r, 32), at] * inverse
            out[a][pl.ds(pl.multiple_of(s * rows + r, 32), 32), at] = value.astype(out_g.dtype)
            return carry

        lax.fori_loop(0, nr // 32, one, 0)

    def keep_factor(a, q, factor):
        for i in range(factor.shape[1] // LANES):
            k = q // LANES + i
            fac[a][k : k + 1, :] = factor[:, i * LANES : (i + 1) * LANES]

    sums0[s] = collapsed(averaged(0, 64, jnp.zeros((8, FIRST), jnp.float32)))

    @pl.when(c == 1)
    def _():
        pl.semaphore_wait(barrier, 7)
        pl.semaphore_signal(go, inc=1, device_id=(mate, m), device_id_type=MESH)

    @pl.when(c == 0)
    def _():
        pl.semaphore_wait(go, 1)

    exchange(0, sums0)
    sums1[s, :, 0:rest] = collapsed(averaged(1, 32, jnp.zeros((8, rest), jnp.float32)))
    upper = averaged(2, 32, jnp.zeros((8, cols), jnp.float32))
    sums1[s, :, rest : rest + cols] = collapsed(averaged(3, 32, upper))
    exchange(1, sums1)

    factor = summed(0, sums0)
    scale(0, 1.0 / factor)
    own(0, 0)
    own(0, 1)
    to_mate(0, s)
    keep_factor(0, 0, factor)

    factors = summed(1, sums1)
    inverses = 1.0 / factors
    inverse = (inverses[:, 0:rest], inverses[:, rest : rest + cols])
    scaled = {0}
    for ur, ul in zip(RIGHT[1:], LEFT[1:]):
        for way, u in ((0, ur), (1, ul)):
            new = u not in scaled
            if new:
                scale(u, inverse[UNITS[u][0]])
                scaled.add(u)
            own(u, way)
            if new:
                to_mate(u, s)
    keep_factor(0, FIRST, factors[:, 0:rest])
    keep_factor(1, 0, factors[:, rest : rest + cols])

    def norm_copy(ref, i, to):
        return pltpu.make_async_remote_copy(
            src_ref=ref, dst_ref=ref, send_sem=nsend.at[i], recv_sem=nrecv.at[i], device_id=to, device_id_type=MESH,
        )

    settle(gains, gain_sem)
    norm1[s] = jnp.zeros((1, LANES), jnp.float32)
    norm1[s, :, 0:32] = gains[0] + gains[1]
    for d in range(1, 4):
        norm_copy(norm1.at[s], 0, (((y + d) % 4) * 2, m)).start()

    @pl.when(c == 1)
    def _():
        norm_copy(norm1.at[s], 0, (mate, m)).start()

    def norm_along_x():
        settle(norm1.at[pl.ds(0, 7)], nrecv.at[0])
        lane_row = lax.broadcasted_iota(jnp.int32, (8, LANES), 0)
        tile = jnp.zeros((8, LANES), jnp.float32)
        for i in range(8):
            tile = jnp.where(lane_row == i, norm1[i], tile)
        norm2[m] = tile
        pl.semaphore_wait(barrier, 6)
        for p in cross_peers[:3]:
            norm_copy(norm2.at[m], 1, (s, p)).start()

    def norm_along_z():
        settle(norm2.at[pl.ds(0, 3)], nrecv.at[1])
        for p in cross_peers[3:]:
            norm_copy(norm2.at[pl.ds(z * 4, 4)], 2, (s, p)).start()

    def norm_to_mate():
        settle(norm2.at[pl.ds(0, 12)], nrecv.at[2])
        for zz in range(4):
            line = norm2[zz * 4]
            for xx in range(1, 4):
                line = line + pltpu.roll(norm2[zz * 4 + xx], 32 * xx, 1)
            norm32[pl.ds(zz, 8, stride=4), :] = line
        norm_copy(norm32, 3, (mate, m)).start()

    steps = [norm_along_x, norm_along_z, norm_to_mate]
    for i, (way, u) in enumerate(by_arrival((0, RIGHT), (1, LEFT))):
        landed(u, way)
        if u in (RELAYED_RIGHT, RELAYED_LEFT)[way]:
            relay(u, way)
        to_mate(u, (left, right)[way])
        if i % 2 and steps:
            pl.when(c == 0)(steps.pop(0))

    @pl.when(c == 1)
    def _():
        norm_copy(norm32, 3, (mate, m)).wait_recv()
        settle(norm1.at[pl.ds(0, 4)], nsend.at[0])

    @pl.when(c == 0)
    def _():
        settle(norm1.at[pl.ds(0, 3)], nsend.at[0])
        settle(norm2.at[pl.ds(0, 3)], nsend.at[1])
        settle(norm2.at[pl.ds(0, 12)], nsend.at[2])
        norm_copy(norm32, 3, (mate, m)).wait_send()

    norm_out[...] = norm32[...].astype(norm_out.dtype)
    settle(sums0.at[pl.ds(0, 7)], ex_send.at[0])
    settle(sums1.at[pl.ds(0, 7)], ex_send.at[1])

    for _, u in by_arrival((0, RELAYED_RIGHT), (1, RELAYED_LEFT)):
        relayed(u)
        to_mate(u, far)

    settle(out_g.at[pl.ds(0, 4 * rows)], own_send)
    settle(out_g.at[pl.ds(0, 2 * rows)], relay_send)
    settle(out_g, mate_recv)
    settle(out_g, mate_send)


def write_kernel(*refs):
    ins, outs, sem = refs[:7], refs[7:14], refs[14]
    copies = []
    for a, b in zip(ins, outs):
        parts = 4 if a.shape[0] % 512 == 0 else 1
        size = a.shape[0] // parts
        for i in range(parts):
            at = pl.ds(i * size, size)
            pltpu.make_async_copy(a.at[at], b.at[at], sem).start()
    for a, b in zip(ins, outs):
        pltpu.make_async_copy(a, b, sem).wait()


def body(tg, sg, tu, su, nt, ns):
    rows, cols = tg.shape
    d_model = rows * 8
    hbm = pl.BlockSpec(memory_space=pltpu.HBM)
    vmem = pl.BlockSpec(memory_space=pltpu.VMEM)
    shapes = (
        ((d_model, cols), jnp.bfloat16),
        ((d_model, cols), jnp.bfloat16),
        ((rows, cols), jnp.float32),
        ((rows, cols), jnp.float32),
        ((cols // LANES, LANES), jnp.float32),
        ((cols // LANES, LANES), jnp.float32),
        ((32, LANES), jnp.bfloat16),
    )
    given = [
        pltpu.with_memory_space_constraint(a, pltpu.HBM)
        for a in (tg, sg, tu, su, nt.reshape(1, 32), ns.reshape(1, 32))
    ]
    gathered = pl.pallas_call(
        gather_kernel,
        out_shape=[pltpu.VMEM(*a) for a in shapes],
        in_specs=[hbm] * 6,
        out_specs=[vmem] * 7,
        scratch_shapes=[
            pltpu.VMEM((2, rows, cols), jnp.float32),
            pltpu.VMEM((2, rows, cols), jnp.float32),
            pltpu.VMEM((2, 1, 32), jnp.float32),
            pltpu.VMEM((8, 1, FIRST), jnp.float32),
            pltpu.VMEM((8, 1, 2 * cols - FIRST), jnp.float32),
            pltpu.VMEM((8, 1, LANES), jnp.float32),
            pltpu.VMEM((16, 8, LANES), jnp.float32),
            pltpu.VMEM((32, LANES), jnp.float32),
            dma((4,)),
            dma(),
            pltpu.SemaphoreType.REGULAR,
            dma((2,)),
            dma((2,)),
            dma(),
            dma((2, len(UNITS))),
            dma(),
            dma((len(UNITS),)),
            dma(),
            dma(),
            dma((4,)),
            dma((4,)),
        ],
        compiler_params=pltpu.CompilerParams(
            collective_id=0, has_side_effects=True, vmem_limit_bytes=32 << 20
        ),
    )(*given)
    g, u, fg, fu, cg, cu, norm = pl.pallas_call(
        write_kernel,
        out_shape=[jax.ShapeDtypeStruct(*a) for a in shapes],
        in_specs=[vmem] * 7,
        out_specs=[hbm] * 7,
        scratch_shapes=[dma()],
        compiler_params=pltpu.CompilerParams(vmem_limit_bytes=16 << 20),
    )(*gathered)
    return g, u, cg.reshape(cols), cu.reshape(cols), norm.reshape(d_model), fg, fu


def solution(mesh):
    spread = P("shard", "model")
    return jax.shard_map(
        body,
        mesh=mesh,
        in_specs=(spread,) * 4 + (P(("shard", "model")),) * 2,
        out_specs=(
            P(None, "model"), P(None, "model"), P("model"), P("model"), P(), spread, spread,
        ),
        check_vma=False,
    )
```

time: 109 us -> 69 us (0.63)
  Pallas kernels: 0 us -> 68.3 us
  blocking collectives: 45 us -> 0 us
  waiting for transfers between devices: 30.7 us -> 0 us
  between operations: 14.8 us -> 0.64 us
  local copies, waits for them, and re-layouts: 13 us -> 0 us
  other arithmetic: 4.91 us -> 0 us
    pallas_call x0 -> x2, Pallas kernels: none -> 68.3 us  [the longest x1 62.8 us: body(): pl.pallas_call(gather_kernel, out_shape=[pltpu.VMEM(*a) for a in shapes],...]
    all_gather x1 -> x0, waiting for transfers between devices: 30.7 us -> none  [sent_together(): filled = lax.all_gather(both, axis, axis=dim, tiled=True)]
    all_gather x3 -> x0, blocking collectives: 27.6 us -> none  [stacked_from(): blocks = lax.all_gather(blocks, axes[k], axis=0, tiled=True)]
    all_to_all x1 -> x0, blocking collectives: 10.5 us -> none  [from_everyone(): return lax.all_to_all(copies, axis, split_axis=0, concat_axis=0, tiled=True)]
    split x1 -> x0, local copies, waits for them, and re-layouts: 10.2 us -> none  [sent_together(): jnp.split(filled, [sum(widths[:k]) for k in range(1, len(widths))], axis=...]
    unnamed x1 -> x0, blocking collectives: 6.85 us -> none
    reduce_sum x2 -> x0, other arithmetic: 3.4 us -> none  [the longest x1 3.36 us: shards(): jnp.sum(jnp.abs(fresh_up), axis=0)]
    unnamed x19 -> x0, local copies, waits for them, and re-layouts: 1.96 us -> none
  transfers between devices with their start and end apart: 1 -> 0, of which waited for: 1 -> 0; matrix products, arithmetic and copies ran while one was open for 2% -> 0% of each run, Pallas kernels for 0% -> 0%
where the time goes in v2:
time: 69 us; the launch traced here: 68.9 us
  Pallas kernels  68.3 us (99%)
    pallas_call x1, Pallas kernels, body(): pl.pallas_call(gather_kernel, out_shape=[pltpu.VMEM(*a) for a in shapes],...  62.8 us
    pallas_call x1, Pallas kernels, body(): pl.pallas_call(write_kernel, out_shape=[jax.ShapeDtypeStruct(*a) for a in...  5.5 us

profile of v2, /device:TPU:1, one launch (start us, length us, event | category | flops | bytes accessed | tf_op | source)
XLA Modules:
  0.0 68.9 jit_solution(10810749832674301509)
XLA Ops:
  0.6 62.8 %shard_map.117 = (bf16[4096,768]{1,0:T(8,128)(2,1)S(1)}, bf16[4096,768]{1,0:T(8,128)(2,1)S(1)}, f32[512,768]{1,0:T(8,128)S(1)}, f32[512,768]{1,0:T(8,128)S(1)}, ...) custom-call(f32[512,768]{1,0:T(8,128)} %tg.1, f32[512,768]{1,0:T(8,128)} %sg.1, ...), custom_call_target="tpu_custom_call" | custom-call | tf_op jit(solution)/shard_map/pallas_call | solution.py:310
  63.4 5.5 %shard_map.118 = (bf16[4096,768]{1,0:T(8,128)(2,1)}, bf16[4096,768]{1,0:T(8,128)(2,1)}, f32[512,768]{1,0:T(8,128)}, f32[512,768]{1,0:T(8,128)}, f32[6,128]{1,0:T...) custom-call(bf16[4096,768]{1,0:T(8,128)(2,1)S(1)} %get-tuple-element.21.refs_0_, ...), custom_call_target="tpu_custom_call" | custom-call | tf_op jit(solution)/shard_map/pallas_call | solution.py:342
